TPU v7x, 512 devices: a whole 4x8x8 slice. The times are simulated.
512 devices in a mesh: dp: 64 (over x, z, core), mp: 8 (over y).
Axes of the slice: x: 4, y: 8, z: 8, core: 2. Of those that a mesh axis runs over, the one named last changes fastest.
Arguments:
- ranges: bfloat16 [8192, 2652], P(('dp', 'mp')), may hold values from 0.0099487305 to 1
- board: int32 [8192, 5], P(('dp', 'mp')), may hold values from 0 to 51, as said below
- targets: bfloat16 [8192, 2652], P(('dp', 'mp')), may hold values from -6 to 6
- w_in: bfloat16 [1536, 2704], P(('mp', 'dp')), may hold values from -0.34570312 to 0.34570312
- w_out: bfloat16 [1536, 2652], P(('mp', 'dp')), may hold values from -0.3046875 to 0.3046875
Outputs:
- predicted: bfloat16 [8192, 2652], P(('dp', 'mp'))
- update_in: float32 [1536, 2704], P(('mp', 'dp'))
- update_out: float32 [1536, 2652], P(('mp', 'dp'))
- loss: float32 [], replicated
Inputs may be any that keep to these rules, and one draw needn't show every extreme that they name: `board`: each row holds 5 different cards.
All inputs are finite; a program needn't handle non-finite values.
Results may differ from a plain program's by a relative error of at most 0.014.
Values may be sent and summed in bfloat16 or wider, within the bound.
A program may use at most 64 MiB of HBM per device.

v0:
```python
import jax
import jax.numpy as jnp
from jax import lax
from jax.sharding import Mesh
from jax.sharding import PartitionSpec as P

CARDS = 52
HIDDEN_SIZE = 1536
DP = ("dp_0", "dp_1", "dp_2")
DP_MP = ("dp_0", "dp_1", "dp_2", "mp")
MP_DP = ("mp", "dp_0", "dp_1", "dp_2")


def laid_out(tiles, dim):
    tiles = jnp.moveaxis(tiles, 0, dim)
    dims = tiles.shape
    return tiles.reshape(*dims[:dim], dims[dim] * dims[dim + 1], *dims[dim + 2 :])


def sent_to_all(array, axis):
    peers = lax.axis_size(axis)
    return lax.all_to_all(
        jnp.broadcast_to(array[None], (peers, *array.shape)), axis, 0, 0, tiled=True
    )


def collect(array, axis, dim):
    return laid_out(sent_to_all(array, axis), dim)


def in_blocks(array, dim, peers):
    before, after = (array.shape[:dim], array.shape[dim + 1 :])
    return jnp.moveaxis(array.reshape(*before, peers, -1, *after), dim, 0)


def sent_and_summed(array, axis, dim):
    peers = lax.axis_size(axis)
    tiles = lax.all_to_all(in_blocks(array, dim, peers), axis, 0, 0, tiled=True)
    return jnp.sum(tiles.astype(jnp.float32), axis=0)


def over_axes(array, axes):
    for axis in axes:
        array = lax.psum(array, axis)
    return array


def huber_terms(error_value):
    magnitude = jnp.abs(error_value)
    return jnp.where(magnitude <= 1.0, 0.5 * error_value * error_value, magnitude - 0.5)


def build_features(all_ranges, all_board, card_count):
    card_ids = jnp.arange(card_count, dtype=jnp.int32)
    onehot_board = jnp.sum(
        (all_board[:, :, None] == card_ids[None, None, :]).astype(jnp.float32), axis=1
    ).astype(jnp.bfloat16)
    return jnp.concatenate([all_ranges, onehot_board], axis=1)


def right_product(left_side, right_block):
    return lax.dot_general(
        left_side, right_block, (((1,), (1,)), ((), ())), preferred_element_type=jnp.float32
    )


def left_product(left_side, right_side):
    return lax.dot_general(
        left_side, right_side, (((0,), (0,)), ((), ())), preferred_element_type=jnp.float32
    )


def body(ranges, board, targets, w_in, w_out):
    mp_count = lax.axis_size("mp")
    dp_count = lax.axis_size(DP)
    stored_rows = ranges.shape[0]
    value_width = w_out.shape[1]
    all_ranges, all_board = (collect(ranges, "mp", 0), collect(board, "mp", 0))
    features = build_features(all_ranges, all_board, CARDS)
    local_in = lax.all_gather(w_in, DP, axis=0, tiled=True)
    preact = right_product(features, local_in)
    hidden = jax.nn.gelu(preact).astype(jnp.bfloat16)
    local_out = lax.all_gather(w_out, DP, axis=0, tiled=True)
    partial_value = jnp.dot(hidden, local_out, preferred_element_type=jnp.float32)
    stacked = partial_value.astype(jnp.bfloat16).reshape(mp_count, stored_rows, value_width)
    received = lax.all_to_all(stacked, "mp", split_axis=0, concat_axis=0, tiled=True)
    summed = jnp.sum(received.astype(jnp.float32), axis=0)
    error_value = summed - targets.astype(jnp.float32)
    own_grad = jnp.clip(error_value, -1.0, 1.0).astype(jnp.bfloat16)
    out_grad = collect(own_grad, "mp", 0)
    predicted = summed.astype(jnp.bfloat16)
    loss_part = jnp.sum(huber_terms(error_value))
    grad_out = sent_and_summed(left_product(hidden, out_grad).astype(jnp.bfloat16), DP, 0)
    hidden_grad = right_product(out_grad, local_out)
    unused_value, gelu_back = jax.vjp(jax.nn.gelu, preact)
    preact_grad = gelu_back(hidden_grad)[0].astype(jnp.bfloat16)
    grad_in = sent_and_summed(left_product(preact_grad, features).astype(jnp.bfloat16), DP, 0)
    square_part = jnp.sum(grad_in * grad_in) + jnp.sum(grad_out * grad_out)
    loss_total, square_total = (over_axes(loss_part, DP_MP), over_axes(square_part, DP_MP))
    count_params = HIDDEN_SIZE * (w_in.shape[1] + value_width)
    scale = lax.rsqrt(square_total / count_params + 1e-06)
    loss = loss_total / (stored_rows * mp_count * dp_count * value_width)
    return (predicted, grad_in * scale, grad_out * scale, loss)


def solution(mesh):
    split = Mesh(mesh.devices.reshape(4, 8, 2, mesh.shape["mp"]), ("dp_0", "dp_1", "dp_2", "mp"))
    placed = (P(DP_MP, None), P(DP_MP, None), P(DP_MP, None), P(MP_DP, None), P(MP_DP, None))
    return jax.shard_map(
        body,
        mesh=split,
        in_specs=placed,
        out_specs=(P(DP_MP, None), P(MP_DP, None), P(MP_DP, None), P()),
        check_vma=False,
    )
```

profile of v0, /device:TPU:8, one launch (start us, length us, event | category | flops | bytes accessed | tf_op | source)
XLA Modules:
  0.0 324.2 jit_solution(1523296444616732126)
XLA Ops:
  0.6 0.7 broadcast_in_dim.7
  1.3 14.7 %all_to_all.30 = s32[8,16,5]{1,2,0:T(8,128)S(1)} all-to-all(s32[8,16,5]{1,2,0:T(8,128)S(1)} %broadcast_in_dim.7), channel_id=1, replica_groups=mesh['dp_0'=4,'dp_1'=8,'dp_2'=2,'mp'=8] {'mp'}, dimensions={0} | all-to-all | bytes 5120 | tf_op jit(solution)/shard_map/all_to_all | solution.py:22
  16.1 1.8 broadcast_in_dim.6
  17.9 4.9 %all-to-all-start = ((bf16[8,16,2652]{2,1,0:T(8,128)(2,1)}), bf16[8,16,2652]{2,1,0:T(8,128)(2,1)S(1)}, u32[]{:S(2)}, u32[]{:S(2)}) async-start(bf16[8,16,2652]{2,1,0:T(8,128)(2,1)} %broadcast_in_dim.6), calls=%async_computation | async-start | bytes 1376256 | tf_op jit(solution)/shard_map/all_to_all | solution.py:22
  22.8 55.9 %all-gather = bf16[64,3,2704]{2,1,0:T(4,128)(2,1)S(1)} all-gather(bf16[1,3,2704]{2,1,0:T(4,128)(2,1)S(1)} %bitcast.17), channel_id=1, replica_groups=mesh['dp_0'=4,'dp_1'=8,'dp_2'=2,'mp'=8] {'dp_0','dp_1','dp_2'}, dimensions={0}, use_global_device_ids=true | all-gather | bytes 1054560 | tf_op jit(solution)/shard_map/all_gather | solution.py:80
  78.7 1.7 reshape.33
  80.4 49.7 %all-gather.1 = bf16[64,3,2652]{2,1,0:T(4,128)(2,1)S(1)} all-gather(bf16[1,3,2652]{2,1,0:T(4,128)(2,1)S(1)} %bitcast.18), channel_id=1, replica_groups=mesh['dp_0'=4,'dp_1'=8,'dp_2'=2,'mp'=8] {'dp_0','dp_1','dp_2'}, dimensions={0}, use_global_device_ids=true | all-gather | bytes 1034280 | tf_op jit(solution)/shard_map/all_gather | solution.py:83
  130.1 0.9 reshape.35
  131.3 1.9 fusion
  133.2 0.7 convolution_convert_fusion.2
  133.9 0.3 copy.18
  134.2 27.2 %all_to_all.31 = bf16[8,16,2652]{2,1,0:T(8,128)(2,1)S(1)} all-to-all(bf16[8,16,2652]{2,1,0:T(8,128)(2,1)S(1)} %bitcast.16), channel_id=1, replica_groups=mesh['dp_0'=4,'dp_1'=8,'dp_2'=2,'mp'=8] {'mp'}, dimensions={0} | all-to-all | bytes 1357824 | tf_op jit(solution)/shard_map/all_to_all | solution.py:86
  161.6 1.3 fusion.2
  162.9 23.8 %all_to_all.32 = bf16[8,16,2652]{2,1,0:T(8,128)(2,1)S(1)} all-to-all(bf16[8,16,2652]{2,1,0:T(8,128)(2,1)S(1)} %broadcast_in_dim.8), channel_id=1, replica_groups=mesh['dp_0'=4,'dp_1'=8,'dp_2'=2,'mp'=8] {'mp'}, dimensions={0} | all-to-all | bytes 1357824 | tf_op jit(solution)/shard_map/all_to_all | solution.py:22
  186.7 0.4 convolution_convert_fusion
  187.1 1.3 reshape.31
  188.4 5.3 %all-to-all-start.5 = ((bf16[64,3,2652]{2,1,0:T(4,128)(2,1)}), bf16[64,3,2652]{2,1,0:T(4,128)(2,1)S(1)}, u32[]{:S(2)}, u32[]{:S(2)}) async-start(bf16[64,3,2652]{2,1,0:T(4,128)(2,1)} %reshape.31), calls=%async_computation.5 | async-start | bytes 2752512 | tf_op jit(solution)/shard_map/all_to_all | solution.py:38
  193.7 3.4 %convolution_convert_fusion.1 = bf16[192,2704]{1,0:T(8,128)(2,1)} fusion(bf16[128,52]{1,0:T(8,128)(2,1)S(1)} %copy.17, bf16[128,2652]{1,0:T(8,128)(2,1)} %bitcast.15, f32[128,192]{0,1:T(8,128)S(1)} %fusion, bf16[128,2652]{1,0:T(8,128)(2,1)S(1)} %bitcast.13, bf16[192,2652]{1,0:T(8,128)(2,1)S(1)} %reshape.35), kind=kOutput, calls=%fused_computation.1 | convolution fusion | flops 265653248 | bytes 3526144 | tf_op jit(solution)/shard_map/dot_general | solution.py:68
  197.1 3.6 %reshape.30 = bf16[64,3,2704]{2,1,0:T(4,128)(2,1)} reshape(bf16[192,2704]{1,0:T(8,128)(2,1)} %convolution_convert_fusion.1) | data formatting | bytes 2076672 | tf_op jit(solution)/shard_map/reshape | solution.py:33
  200.7 27.9 %all-to-all-done.5 = bf16[64,3,2652]{2,1,0:T(4,128)(2,1)S(1)} async-done(((bf16[64,3,2652]{2,1,0:T(4,128)(2,1)}), bf16[64,3,2652]{2,1,0:T(4,128)(2,1)S(1)}, u32[]{:S(2)}, u32[]{:S(2)}) %all-to-all-start.5) | async-done | bytes 1018400 | tf_op jit(solution)/shard_map/all_to_all | solution.py:38
  228.6 6.8 %all-to-all-start.4 = ((bf16[64,3,2704]{2,1,0:T(4,128)(2,1)}), bf16[64,3,2704]{2,1,0:T(4,128)(2,1)S(1)}, u32[]{:S(2)}, u32[]{:S(2)}) async-start(bf16[64,3,2704]{2,1,0:T(4,128)(2,1)} %reshape.30), calls=%async_computation.4 | async-start | bytes 2883584 | tf_op jit(solution)/shard_map/all_to_all | solution.py:38
  235.4 0.6 convert_reduce_fusion.1
  236.0 0.6 multiply_reduce_fusion.1
  236.6 35.1 %all-to-all-done.4 = bf16[64,3,2704]{2,1,0:T(4,128)(2,1)S(1)} async-done(((bf16[64,3,2704]{2,1,0:T(4,128)(2,1)}), bf16[64,3,2704]{2,1,0:T(4,128)(2,1)S(1)}, u32[]{:S(2)}, u32[]{:S(2)}) %all-to-all-start.4) | async-done | bytes 1038368 | tf_op jit(solution)/shard_map/all_to_all | solution.py:38
  271.7 0.6 convert_reduce_fusion
  272.3 0.6 multiply_reduce_fusion
  274.2 10.1 %all-reduce.2 = (f32[]{:T(128)}, f32[]{:T(128)}) all-reduce(f32[]{:T(128)S(6)} %add.34, f32[]{:T(128)} %get-tuple-element.12), channel_id=1, replica_groups=mesh['dp_0'=4,'dp_1'=8,'dp_2'=2,'mp'=8] {'dp_0'}, use_global_device_ids=true, to_apply=%region_6.7 | all-reduce | flops 2 | bytes 16 | tf_op jit(solution)/shard_map/psum | solution.py:44
  284.3 16.9 %all-reduce.1 = (f32[]{:T(128)}, f32[]{:T(128)}) all-reduce(f32[]{:T(128)} %get-tuple-element.8, f32[]{:T(128)} %get-tuple-element.9), channel_id=1, replica_groups=mesh['dp_0'=4,'dp_1'=8,'dp_2'=2,'mp'=8] {'dp_1'}, use_global_device_ids=true, to_apply=%region_7.8 | all-reduce | flops 2 | bytes 16 | tf_op jit(solution)/shard_map/psum | solution.py:44
  301.2 3.1 all-reduce.3
  304.2 16.2 %all-reduce = (f32[]{:T(128)}, f32[]{:T(128)}) all-reduce(f32[]{:T(128)} %get-tuple-element.10, f32[]{:T(128)} %get-tuple-element.11), channel_id=1, replica_groups=mesh['dp_0'=4,'dp_1'=8,'dp_2'=2,'mp'=8] {'mp'}, use_global_device_ids=true, to_apply=%region_9.10 | all-reduce | flops 2 | bytes 16 | tf_op jit(solution)/shard_map/psum | solution.py:44
  321.2 0.6 broadcast_multiply_fusion.1
  321.8 0.6 broadcast_multiply_fusion
  (15 shorter events, 0.4 us)
Async XLA Ops:
  0.6 22.1 %copy-start.2 = (bf16[3,2704]{1,0:T(4,128)(2,1)S(1)}, bf16[3,2704]{1,0:T(4,128)(2,1)}, u32[]{:S(2)}) copy-start(bf16[3,2704]{1,0:T(4,128)(2,1)} %param.8) | copy-start | bytes 48676
  17.9 113.4 %all-to-all-start = ((bf16[8,16,2652]{2,1,0:T(8,128)(2,1)}), bf16[8,16,2652]{2,1,0:T(8,128)(2,1)S(1)}, u32[]{:S(2)}, u32[]{:S(2)}) async-start(bf16[8,16,2652]{2,1,0:T(8,128)(2,1)} %broadcast_in_dim.6), calls=%async_computation | async-start | bytes 1376256 | tf_op jit(solution)/shard_map/all_to_all | solution.py:22
  78.6 1.7 copy-start.3
  131.3 31.7 %copy-start = (bf16[8,16,2652]{2,1,0:T(8,128)(2,1)}, bf16[8,16,2652]{2,1,0:T(8,128)(2,1)S(1)}, u32[]{:S(2)}) copy-start(bf16[8,16,2652]{2,1,0:T(8,128)(2,1)S(1)} %all-to-all-done) | copy-start | bytes 2036740
  134.2 27.3 %copy-start.1 = (bf16[16,2652]{1,0:T(8,128)(2,1)S(1)}, bf16[16,2652]{1,0:T(8,128)(2,1)}, u32[]{:S(2)}) copy-start(bf16[16,2652]{1,0:T(8,128)(2,1)} %param.7) | copy-start | bytes 254596
  188.4 40.1 %all-to-all-start.5 = ((bf16[64,3,2652]{2,1,0:T(4,128)(2,1)}), bf16[64,3,2652]{2,1,0:T(4,128)(2,1)S(1)}, u32[]{:S(2)}, u32[]{:S(2)}) async-start(bf16[64,3,2652]{2,1,0:T(4,128)(2,1)} %reshape.31), calls=%async_computation.5 | async-start | bytes 2752512 | tf_op jit(solution)/shard_map/all_to_all | solution.py:38
  228.6 43.1 %all-to-all-start.4 = ((bf16[64,3,2704]{2,1,0:T(4,128)(2,1)}), bf16[64,3,2704]{2,1,0:T(4,128)(2,1)S(1)}, u32[]{:S(2)}, u32[]{:S(2)}) async-start(bf16[64,3,2704]{2,1,0:T(4,128)(2,1)} %reshape.30), calls=%async_computation.4 | async-start | bytes 2883584 | tf_op jit(solution)/shard_map/all_to_all | solution.py:38
where the time goes:
time: 325 us; the launch traced here: 324 us
  blocking collectives  218 us (67%)
  waiting for transfers between devices  62.9 us (19%)
  starting transfers between devices  17 us (5%)
  local copies, waits for them, and re-layouts  10.7 us (3%)
  matrix products  6.4 us (2%)
  other arithmetic  5.09 us (2%)
  between operations  4.52 us (1%)
    all_to_all x2, waiting for transfers between devices, sent_and_summed(): tiles = lax.all_to_all(in_blocks(array, dim, peers), axis, 0, 0, tiled=True)  62.9 us
    all_gather x1, blocking collectives, body(): local_in = lax.all_gather(w_in, DP, axis=0, tiled=True)  55.9 us
    all_gather x1, blocking collectives, body(): local_out = lax.all_gather(w_out, DP, axis=0, tiled=True)  49.7 us
    psum x4, blocking collectives, over_axes(): array = lax.psum(array, axis)  46.3 us
    all_to_all x2, blocking collectives, sent_to_all(): lax.all_to_all(jnp.broadcast_to(array[None], (peers, *array.shape)), axis...  38.5 us
    all_to_all x1, blocking collectives, body(): lax.all_to_all(stacked, 'mp', split_axis=0, concat_axis=0, tiled=True)  27.2 us
    all_to_all x2, starting transfers between devices, sent_and_summed(): tiles = lax.all_to_all(in_blocks(array, dim, peers), axis, 0, 0, tiled=True)  12.1 us
  transfers between devices with their start and end apart: 3, of which 2 were waited for; matrix products, arithmetic and copies ran while one was open for 3% of the time, Pallas kernels for 0%

commit v1 on v0

--- a/solution.py
+++ b/solution.py
@@ -77,7 +77,9 @@
     value_width = w_out.shape[1]
     all_ranges, all_board = (collect(ranges, "mp", 0), collect(board, "mp", 0))
     features = build_features(all_ranges, all_board, CARDS)
-    local_in = lax.all_gather(w_in, DP, axis=0, tiled=True)
+    local_in = jnp.concatenate(
+        lax.all_to_all(jnp.stack([w_in] * lax.axis_size(DP)), DP, 0, 0), axis=0
+    )
     preact = right_product(features, local_in)
     hidden = jax.nn.gelu(preact).astype(jnp.bfloat16)
     local_out = lax.all_gather(w_out, DP, axis=0, tiled=True)

time: 325 us -> 327 us (level)
    all_gather x1 -> x0, blocking collectives: 55.9 us -> none  [body(): local_in = lax.all_gather(w_in, DP, axis=0, tiled=True)]
    all_to_all x0 -> x1, blocking collectives: none -> 49.2 us  [body(): lax.all_to_all(jnp.stack([w_in] * lax.axis_size(DP)), DP, 0, 0)]
    all_gather x1, blocking collectives: 49.7 us -> 54 us  [body(): local_out = lax.all_gather(w_out, DP, axis=0, tiled=True)]
  transfers between devices with their start and end apart: 3 -> 3, of which waited for: 2 -> 2; matrix products, arithmetic and copies ran while one was open for 3% -> 4% of each run, Pallas kernels for 0% -> 0%
where the time goes in v1:
time: 327 us; the launch traced here: 326 us
  blocking collectives  215 us (66%)
  waiting for transfers between devices  62.9 us (19%)
  starting transfers between devices  18.9 us (6%)
  local copies, waits for them, and re-layouts  12.6 us (4%)
  matrix products  6.4 us (2%)
  other arithmetic  5.09 us (2%)
  between operations  4.51 us (1%)
    all_to_all x2, waiting for transfers between devices, sent_and_summed(): tiles = lax.all_to_all(in_blocks(array, dim, peers), axis, 0, 0, tiled=True)  62.9 us
    all_gather x1, blocking collectives, body(): local_out = lax.all_gather(w_out, DP, axis=0, tiled=True)  54 us
    all_to_all x1, blocking collectives, body(): lax.all_to_all(jnp.stack([w_in] * lax.axis_size(DP)), DP, 0, 0)  49.2 us
    psum x4, blocking collectives, over_axes(): array = lax.psum(array, axis)  46.3 us
    all_to_all x2, blocking collectives, sent_to_all(): lax.all_to_all(jnp.broadcast_to(array[None], (peers, *array.shape)), axis...  38.5 us
    all_to_all x1, blocking collectives, body(): lax.all_to_all(stacked, 'mp', split_axis=0, concat_axis=0, tiled=True)  27.2 us
    all_to_all x2, starting transfers between devices, sent_and_summed(): tiles = lax.all_to_all(in_blocks(array, dim, peers), axis, 0, 0, tiled=True)  14 us
  transfers between devices with their start and end apart: 3, of which 2 were waited for; matrix products, arithmetic and copies ran while one was open for 4% of the time, Pallas kernels for 0%

profile of v1, /device:TPU:8, one launch (start us, length us, event | category | flops | bytes accessed | tf_op | source)
XLA Modules:
  0.0 325.6 jit_solution(6803625176636629023)
XLA Ops:
  0.6 0.7 broadcast_in_dim.7
  1.3 14.7 %all_to_all.35 = s32[8,16,5]{1,2,0:T(8,128)S(1)} all-to-all(s32[8,16,5]{1,2,0:T(8,128)S(1)} %broadcast_in_dim.7), channel_id=1, replica_groups=mesh['dp_0'=4,'dp_1'=8,'dp_2'=2,'mp'=8] {'mp'}, dimensions={0} | all-to-all | bytes 5120 | tf_op jit(solution)/shard_map/all_to_all | solution.py:22
  16.0 1.1 stack.2
  17.2 49.2 %all_to_all.36 = bf16[64,3,2704]{2,1,0:T(4,128)(2,1)S(1)} all-to-all(bf16[64,3,2704]{2,1,0:T(4,128)(2,1)S(1)} %stack.2), channel_id=1, replica_groups=mesh['dp_0'=4,'dp_1'=8,'dp_2'=2,'mp'=8] {'dp_0','dp_1','dp_2'}, dimensions={0} | all-to-all | bytes 2076672 | tf_op jit(solution)/shard_map/all_to_all | solution.py:81
  66.3 0.9 broadcast_in_dim.6
  67.2 4.9 %all-to-all-start = ((bf16[8,16,2652]{2,1,0:T(8,128)(2,1)}), bf16[8,16,2652]{2,1,0:T(8,128)(2,1)S(1)}, u32[]{:S(2)}, u32[]{:S(2)}) async-start(bf16[8,16,2652]{2,1,0:T(8,128)(2,1)} %broadcast_in_dim.6), calls=%async_computation | async-start | bytes 1376256 | tf_op jit(solution)/shard_map/all_to_all | solution.py:22
  72.1 54.0 %all-gather = bf16[64,3,2652]{2,1,0:T(4,128)(2,1)} all-gather(bf16[1,3,2652]{2,1,0:T(4,128)(2,1)S(1)} %bitcast.16), channel_id=1, replica_groups=mesh['dp_0'=4,'dp_1'=8,'dp_2'=2,'mp'=8] {'dp_0','dp_1','dp_2'}, dimensions={0}, use_global_device_ids=true | all-gather | bytes 1034280 | tf_op jit(solution)/shard_map/all_gather | solution.py:85
  126.2 2.6 reshape.39
  129.0 1.7 reshape.33
  130.8 1.9 fusion
  132.7 0.7 convolution_convert_fusion.2
  133.7 27.2 %all_to_all.37 = bf16[8,16,2652]{2,1,0:T(8,128)(2,1)S(1)} all-to-all(bf16[8,16,2652]{2,1,0:T(8,128)(2,1)S(1)} %bitcast.15), channel_id=1, replica_groups=mesh['dp_0'=4,'dp_1'=8,'dp_2'=2,'mp'=8] {'mp'}, dimensions={0} | all-to-all | bytes 1357824 | tf_op jit(solution)/shard_map/all_to_all | solution.py:88
  161.1 1.3 fusion.2
  162.4 23.8 %all_to_all.38 = bf16[8,16,2652]{2,1,0:T(8,128)(2,1)S(1)} all-to-all(bf16[8,16,2652]{2,1,0:T(8,128)(2,1)S(1)} %broadcast_in_dim.8), channel_id=1, replica_groups=mesh['dp_0'=4,'dp_1'=8,'dp_2'=2,'mp'=8] {'mp'}, dimensions={0} | all-to-all | bytes 1357824 | tf_op jit(solution)/shard_map/all_to_all | solution.py:22
  186.2 0.4 convolution_convert_fusion
  186.6 1.3 reshape.37
  187.9 7.2 %all-to-all-start.6 = ((bf16[64,3,2652]{2,1,0:T(4,128)(2,1)}), bf16[64,3,2652]{2,1,0:T(4,128)(2,1)S(1)}, u32[]{:S(2)}, u32[]{:S(2)}) async-start(bf16[64,3,2652]{2,1,0:T(4,128)(2,1)} %reshape.37), calls=%async_computation.6 | async-start | bytes 2752512 | tf_op jit(solution)/shard_map/all_to_all | solution.py:38
  195.1 3.4 %convolution_convert_fusion.1 = bf16[192,2704]{1,0:T(8,128)(2,1)} fusion(bf16[128,52]{1,0:T(8,128)(2,1)S(1)} %copy.17, bf16[128,2652]{1,0:T(8,128)(2,1)} %bitcast.14, f32[128,192]{0,1:T(8,128)S(1)} %fusion, bf16[128,2652]{1,0:T(8,128)(2,1)S(1)} %bitcast.12, bf16[192,2652]{1,0:T(8,128)(2,1)S(1)} %reshape.39), kind=kOutput, calls=%fused_computation.1 | convolution fusion | flops 265653248 | bytes 3526144 | tf_op jit(solution)/shard_map/dot_general | solution.py:68
  198.5 3.6 %reshape.36 = bf16[64,3,2704]{2,1,0:T(4,128)(2,1)} reshape(bf16[192,2704]{1,0:T(8,128)(2,1)} %convolution_convert_fusion.1) | data formatting | bytes 2076672 | tf_op jit(solution)/shard_map/reshape | solution.py:33
  202.1 27.9 %all-to-all-done.6 = bf16[64,3,2652]{2,1,0:T(4,128)(2,1)S(1)} async-done(((bf16[64,3,2652]{2,1,0:T(4,128)(2,1)}), bf16[64,3,2652]{2,1,0:T(4,128)(2,1)S(1)}, u32[]{:S(2)}, u32[]{:S(2)}) %all-to-all-start.6) | async-done | bytes 1018400 | tf_op jit(solution)/shard_map/all_to_all | solution.py:38
  230.0 6.8 %all-to-all-start.5 = ((bf16[64,3,2704]{2,1,0:T(4,128)(2,1)}), bf16[64,3,2704]{2,1,0:T(4,128)(2,1)S(1)}, u32[]{:S(2)}, u32[]{:S(2)}) async-start(bf16[64,3,2704]{2,1,0:T(4,128)(2,1)} %reshape.36), calls=%async_computation.5 | async-start | bytes 2883584 | tf_op jit(solution)/shard_map/all_to_all | solution.py:38
  236.8 0.6 convert_reduce_fusion.1
  237.4 0.6 multiply_reduce_fusion.1
  238.0 35.1 %all-to-all-done.5 = bf16[64,3,2704]{2,1,0:T(4,128)(2,1)S(1)} async-done(((bf16[64,3,2704]{2,1,0:T(4,128)(2,1)}), bf16[64,3,2704]{2,1,0:T(4,128)(2,1)S(1)}, u32[]{:S(2)}, u32[]{:S(2)}) %all-to-all-start.5) | async-done | bytes 1038368 | tf_op jit(solution)/shard_map/all_to_all | solution.py:38
  273.1 0.6 convert_reduce_fusion
  273.7 0.6 multiply_reduce_fusion
  275.6 10.1 %all-reduce.2 = (f32[]{:T(128)}, f32[]{:T(128)}) all-reduce(f32[]{:T(128)S(6)} %add.34, f32[]{:T(128)} %get-tuple-element.12), channel_id=1, replica_groups=mesh['dp_0'=4,'dp_1'=8,'dp_2'=2,'mp'=8] {'dp_0'}, use_global_device_ids=true, to_apply=%region_6.7 | all-reduce | flops 2 | bytes 16 | tf_op jit(solution)/shard_map/psum | solution.py:44
  285.7 16.9 %all-reduce.1 = (f32[]{:T(128)}, f32[]{:T(128)}) all-reduce(f32[]{:T(128)} %get-tuple-element.8, f32[]{:T(128)} %get-tuple-element.9), channel_id=1, replica_groups=mesh['dp_0'=4,'dp_1'=8,'dp_2'=2,'mp'=8] {'dp_1'}, use_global_device_ids=true, to_apply=%region_7.8 | all-reduce | flops 2 | bytes 16 | tf_op jit(solution)/shard_map/psum | solution.py:44
  302.6 3.1 all-reduce.3
  305.7 16.2 %all-reduce = (f32[]{:T(128)}, f32[]{:T(128)}) all-reduce(f32[]{:T(128)} %get-tuple-element.10, f32[]{:T(128)} %get-tuple-element.11), channel_id=1, replica_groups=mesh['dp_0'=4,'dp_1'=8,'dp_2'=2,'mp'=8] {'mp'}, use_global_device_ids=true, to_apply=%region_9.10 | all-reduce | flops 2 | bytes 16 | tf_op jit(solution)/shard_map/psum | solution.py:44
  322.6 0.6 broadcast_multiply_fusion.1
  323.2 0.6 broadcast_multiply_fusion
  (16 shorter events, 0.7 us)
Async XLA Ops:
  17.1 49.2 %copy-start.1 = (bf16[16,2652]{1,0:T(8,128)(2,1)S(1)}, bf16[16,2652]{1,0:T(8,128)(2,1)}, u32[]{:S(2)}) copy-start(bf16[16,2652]{1,0:T(8,128)(2,1)} %param.5) | copy-start | bytes 254596
  66.3 5.8 %copy-start.3 = (bf16[3,2652]{1,0:T(4,128)(2,1)S(1)}, bf16[3,2652]{1,0:T(4,128)(2,1)}, u32[]{:S(2)}) copy-start(bf16[3,2652]{1,0:T(4,128)(2,1)} %param.9) | copy-start | bytes 47740
  67.2 63.5 %all-to-all-start = ((bf16[8,16,2652]{2,1,0:T(8,128)(2,1)}), bf16[8,16,2652]{2,1,0:T(8,128)(2,1)S(1)}, u32[]{:S(2)}, u32[]{:S(2)}) async-start(bf16[8,16,2652]{2,1,0:T(8,128)(2,1)} %broadcast_in_dim.6), calls=%async_computation | async-start | bytes 1376256 | tf_op jit(solution)/shard_map/all_to_all | solution.py:22
  130.8 31.6 %copy-start = (bf16[8,16,2652]{2,1,0:T(8,128)(2,1)}, bf16[8,16,2652]{2,1,0:T(8,128)(2,1)S(1)}, u32[]{:S(2)}) copy-start(bf16[8,16,2652]{2,1,0:T(8,128)(2,1)S(1)} %all-to-all-done) | copy-start | bytes 2036740
  133.7 27.3 %copy-start.2 = (bf16[16,2652]{1,0:T(8,128)(2,1)S(1)}, bf16[16,2652]{1,0:T(8,128)(2,1)}, u32[]{:S(2)}) copy-start(bf16[16,2652]{1,0:T(8,128)(2,1)} %param.7) | copy-start | bytes 254596
  187.9 42.1 %all-to-all-start.6 = ((bf16[64,3,2652]{2,1,0:T(4,128)(2,1)}), bf16[64,3,2652]{2,1,0:T(4,128)(2,1)S(1)}, u32[]{:S(2)}, u32[]{:S(2)}) async-start(bf16[64,3,2652]{2,1,0:T(4,128)(2,1)} %reshape.37), calls=%async_computation.6 | async-start | bytes 2752512 | tf_op jit(solution)/shard_map/all_to_all | solution.py:38
  230.0 43.1 %all-to-all-start.5 = ((bf16[64,3,2704]{2,1,0:T(4,128)(2,1)}), bf16[64,3,2704]{2,1,0:T(4,128)(2,1)S(1)}, u32[]{:S(2)}, u32[]{:S(2)}) async-start(bf16[64,3,2704]{2,1,0:T(4,128)(2,1)} %reshape.36), calls=%async_computation.5 | async-start | bytes 2883584 | tf_op jit(solution)/shard_map/all_to_all | solution.py:38
